TPU v7x, 32 devices: a whole 2x2x4 slice. The times are simulated.
32 devices in a mesh: wide: 8 (over z, x), narrow: 4 (over y, core).
Axes of the slice: x: 2, y: 2, z: 4, core: 2. Of those that a mesh axis runs over, the one named last changes fastest.
Arguments:
- tokens: bfloat16 [3, 10240, 768], P(None, 'wide'), may hold values from -6 to 6
- image_lengths: int32 [3, 8, 8], P(None, 'wide'), may hold values from 1 to 196, 1280 in all within a row
- heads_weight: bfloat16 [768, 3, 768], P('wide', None, 'narrow'), may hold values from -0.21875 to 0.21875
- heads_bias: float32 [2, 768], P(None, 'narrow'), may hold values from -3 to 3
- out_weight: bfloat16 [768, 768], P('narrow', 'wide'), may hold values from -1.75 to 1.75
- out_bias: float32 [768], replicated, may hold values from -3 to 3
- up_weight: bfloat16 [768, 3072], P('wide', 'narrow'), may hold values from -0.21875 to 0.21875
- up_bias: float32 [3072], P('narrow'), may hold values from -3 to 3
- down_weight: bfloat16 [3072, 768], P('narrow', 'wide'), may hold values from -0.109375 to 0.109375
- down_bias: float32 [768], replicated, may hold values from -3 to 3
- first_gain: float32 [768], replicated, may hold values from 0.1 to 1.9
- first_shift: float32 [768], replicated, may hold values from -3 to 3
- second_gain: float32 [768], replicated, may hold values from 0.1 to 1.9
- second_shift: float32 [768], replicated, may hold values from -3 to 3
- mixer_scale: float32 [768], replicated, may hold values from 0.5 to 2
- feed_scale: float32 [768], replicated, may hold values from 0.5 to 2
- cotangent: bfloat16 [3, 10240, 768], P(None, 'wide'), may hold values from -6 to 6
Outputs:
- layer_out: bfloat16 [3, 10240, 768], P(None, 'wide')
- token_grad: bfloat16 [3, 10240, 768], P(None, ('wide', 'narrow'))
- heads_weight_grad: float32 [768, 3, 768], P(None, None, 'narrow')
- heads_bias_grad: float32 [2, 768], P(None, 'narrow')
- out_weight_grad: float32 [768, 768], P('narrow')
- out_bias_grad: float32 [768], replicated
- up_weight_grad: float32 [768, 3072], P(None, 'narrow')
- up_bias_grad: float32 [3072], P('narrow')
- down_weight_grad: float32 [3072, 768], P('narrow')
- down_bias_grad: float32 [768], replicated
- first_gain_grad: float32 [768], replicated
- first_shift_grad: float32 [768], replicated
- second_gain_grad: float32 [768], replicated
- second_shift_grad: float32 [768], replicated
- mixer_scale_grad: float32 [768], replicated
- feed_scale_grad: float32 [768], replicated
Inputs may be any that keep to these rules, and one draw needn't show every extreme that they name: `image_lengths`: each row of 8 numbers gives the lengths of the images packed in order into one micro-batch of one index of wide; they sum to 1280, and the largest is 196.
All inputs are finite; a program needn't handle non-finite values.
Results may differ from a plain program's by a relative error of at most 0.02.
Values may be sent and summed in bfloat16 or wider, within the bound.
No kernel may reach another device: no remote copies, remote signals or barrier semaphores. Data moves between devices by JAX's collectives and lax.ppermute only.
A program may use at most 256 MiB of HBM per device.

v0:
```python
from functools import partial
from functools import reduce
import jax
import jax.numpy as jnp
from jax import lax
from jax.sharding import PartitionSpec as P

HEAD_DIM = 64
QUERY_BLOCK = 640
epsilon = 1e-06


def norm_parts(values_in):
    center = jnp.mean(values_in, axis=-1, keepdims=True)
    shifted = values_in - center
    inverse = lax.rsqrt(jnp.mean(shifted * shifted, axis=-1, keepdims=True) + epsilon)
    return (shifted * inverse, inverse)


def norm_back(grad_in, unit_rows, inverse, gain_row):
    scaled = grad_in * gain_row
    return inverse * (
        scaled
        - jnp.mean(scaled, axis=-1, keepdims=True)
        - unit_rows * jnp.mean(scaled * unit_rows, axis=-1, keepdims=True)
    )


def image_index(sizes_row, row_count):
    bounds = jnp.cumsum(sizes_row)
    places = jnp.arange(row_count, dtype=jnp.int32)
    return jnp.sum((places[:, None] >= bounds[None, :]).astype(jnp.int32), axis=1)


def exact_gelu(values_in):
    return jax.nn.gelu(values_in, approximate=False)


def attend_forward(key_heads, value_heads, attention_scale, block_items):
    query_heads, same_image = block_items
    raw_scores = (
        jnp.einsum("qhc,khc->hqk", query_heads, key_heads, preferred_element_type=jnp.float32)
        * attention_scale
    )
    scores = jnp.where(same_image[None], raw_scores, -1e30)
    row_max = jnp.max(scores, axis=-1, keepdims=True)
    exp_scores = jnp.exp(scores - row_max)
    exp_total = jnp.sum(exp_scores, axis=-1, keepdims=True)
    soft_weights = (exp_scores / exp_total).astype(jnp.bfloat16)
    context = jnp.einsum(
        "hqk,khc->qhc", soft_weights, value_heads, preferred_element_type=jnp.float32
    )
    return (context, row_max + jnp.log(exp_total))


def attend_back(key_heads, value_heads, attention_scale, running, block_items):
    query_heads, context_grad, same_image, log_total = block_items
    raw_scores = (
        jnp.einsum("qhc,khc->hqk", query_heads, key_heads, preferred_element_type=jnp.float32)
        * attention_scale
    )
    scores = jnp.where(same_image[None], raw_scores, -1e30)
    soft_weights = jnp.exp(scores - log_total)
    weight_grad = jnp.einsum(
        "qhc,khc->hqk", context_grad, value_heads, preferred_element_type=jnp.float32
    )
    row_delta = jnp.sum(soft_weights * weight_grad, axis=-1, keepdims=True)
    score_grad = (soft_weights * (weight_grad - row_delta)).astype(jnp.bfloat16)
    query_grad = (
        jnp.einsum("hqk,khc->qhc", score_grad, key_heads, preferred_element_type=jnp.float32)
        * attention_scale
    )
    key_grad = (
        jnp.einsum("hqk,qhc->khc", score_grad, query_heads, preferred_element_type=jnp.float32)
        * attention_scale
    )
    value_grad = jnp.einsum(
        "hqk,qhc->khc",
        soft_weights.astype(jnp.bfloat16),
        context_grad,
        preferred_element_type=jnp.float32,
    )
    return ((running[0] + key_grad, running[1] + value_grad), query_grad)


def feed_term(upper_grad, up_full):
    return jnp.einsum("rf,df->rd", upper_grad, up_full, preferred_element_type=jnp.float32)


def heads_term_rows(heads_grad, heads_full):
    return jnp.einsum("rtc,dtc->rd", heads_grad, heads_full, preferred_element_type=jnp.float32)


def add_tuples(left, right):
    return jax.tree.map(jnp.add, left, right)


def body(
    tokens,
    image_lengths,
    heads_weight,
    heads_bias,
    out_weight,
    out_bias,
    up_weight,
    up_bias,
    down_weight,
    down_bias,
    first_gain,
    first_shift,
    second_gain,
    second_shift,
    mixer_scale,
    feed_scale,
    cotangent,
):
    micro_count, row_count, width = tokens.shape
    quarter = row_count // lax.axis_size("narrow")
    quarter_start = lax.axis_index("narrow") * quarter
    attention_scale = HEAD_DIM ** (-0.5)
    head_local = heads_weight.shape[2] // HEAD_DIM
    block_count = row_count // QUERY_BLOCK

    def quarter_rows(values_in):
        return lax.dynamic_slice_in_dim(values_in, quarter_start, quarter, 0)

    zero_row = jnp.zeros((width,), jnp.float32)
    out_bias_sum, down_bias_sum = (zero_row, zero_row)
    first_gain_sum, first_shift_sum = (zero_row, zero_row)
    second_gain_sum, second_shift_sum = (zero_row, zero_row)
    mixer_scale_sum, feed_scale_sum = (zero_row, zero_row)
    head_bias_sum = jnp.zeros(heads_bias.shape, jnp.float32)
    up_bias_sum = jnp.zeros(up_bias.shape, jnp.float32)
    term_list = []
    outputs = []
    input_grads = []
    for micro_index in range(micro_count):
        gathered = (
            lax.all_gather(heads_weight, "wide", axis=0, tiled=True),
            lax.all_gather(out_weight, "wide", axis=1, tiled=True),
            lax.all_gather(up_weight, "wide", axis=0, tiled=True),
            lax.all_gather(down_weight, "wide", axis=1, tiled=True),
        )
        heads_full, out_full, up_full, down_full = gathered
        token_rows = tokens[micro_index].astype(jnp.float32)
        index_row = image_index(image_lengths[micro_index, 0], row_count)
        same_image = index_row[:, None] == index_row[None, :]
        first_unit, first_inverse = norm_parts(token_rows)
        first_normed = (first_unit * first_gain + first_shift).astype(jnp.bfloat16)
        projected = jnp.einsum(
            "rd,dtc->rtc", first_normed, heads_full, preferred_element_type=jnp.float32
        )
        query_heads = (
            (projected[:, 0] + heads_bias[0])
            .astype(jnp.bfloat16)
            .reshape(row_count, head_local, HEAD_DIM)
        )
        key_heads = projected[:, 1].astype(jnp.bfloat16).reshape(row_count, head_local, HEAD_DIM)
        value_heads = (
            (projected[:, 2] + heads_bias[1])
            .astype(jnp.bfloat16)
            .reshape(row_count, head_local, HEAD_DIM)
        )
        query_blocks = query_heads.reshape(block_count, QUERY_BLOCK, head_local, HEAD_DIM)
        same_blocks = same_image.reshape(block_count, QUERY_BLOCK, row_count)
        context_blocks, log_total = lax.map(
            partial(attend_forward, key_heads, value_heads, attention_scale),
            (query_blocks, same_blocks),
        )
        context = context_blocks.reshape(row_count, head_local * HEAD_DIM).astype(jnp.bfloat16)
        mixed = lax.psum(
            jnp.dot(context, out_full, preferred_element_type=jnp.float32).astype(jnp.bfloat16),
            "narrow",
        ).astype(jnp.float32)
        middle = token_rows + mixer_scale * (mixed + out_bias)
        second_unit, second_inverse = norm_parts(middle)
        second_normed = (second_unit * second_gain + second_shift).astype(jnp.bfloat16)
        upper = jnp.dot(second_normed, up_full, preferred_element_type=jnp.float32) + up_bias
        active, gelu_slope = jax.vjp(exact_gelu, upper)
        active = active.astype(jnp.bfloat16)
        feed = lax.psum(
            jnp.dot(active, down_full, preferred_element_type=jnp.float32).astype(jnp.bfloat16),
            "narrow",
        ).astype(jnp.float32)
        outputs.append((middle + feed_scale * (feed + down_bias)).astype(jnp.bfloat16))
        output_grad = cotangent[micro_index].astype(jnp.float32)
        feed_grad = (feed_scale * output_grad).astype(jnp.bfloat16)
        active_grad = jnp.einsum(
            "rd,fd->rf", feed_grad, down_full, preferred_element_type=jnp.float32
        )
        down_term = jnp.einsum("rf,rd->fd", active, feed_grad, preferred_element_type=jnp.float32)
        upper_grad = gelu_slope(active_grad)[0].astype(jnp.bfloat16)
        up_term = jnp.einsum(
            "rd,rf->df", second_normed, upper_grad, preferred_element_type=jnp.float32
        )
        up_bias_sum = up_bias_sum + jnp.sum(upper_grad.astype(jnp.float32), axis=0)
        second_normed_grad = lax.psum_scatter(
            feed_term(upper_grad, up_full).astype(jnp.bfloat16),
            "narrow",
            scatter_dimension=0,
            tiled=True,
        ).astype(jnp.float32)
        out_quarter = quarter_rows(output_grad)
        second_unit_part = quarter_rows(second_unit)
        second_gain_sum = second_gain_sum + jnp.sum(second_normed_grad * second_unit_part, axis=0)
        second_shift_sum = second_shift_sum + jnp.sum(second_normed_grad, axis=0)
        feed_scale_sum = feed_scale_sum + jnp.sum(
            out_quarter * (quarter_rows(feed) + down_bias), axis=0
        )
        down_bias_sum = down_bias_sum + feed_scale * jnp.sum(out_quarter, axis=0)
        middle_grad = out_quarter + norm_back(
            second_normed_grad, second_unit_part, quarter_rows(second_inverse), second_gain
        )
        mixer_scale_sum = mixer_scale_sum + jnp.sum(
            middle_grad * (quarter_rows(mixed) + out_bias), axis=0
        )
        out_bias_sum = out_bias_sum + mixer_scale * jnp.sum(middle_grad, axis=0)
        mixed_grad = lax.all_gather(
            (mixer_scale * middle_grad).astype(jnp.bfloat16), "narrow", axis=0, tiled=True
        )
        out_term = jnp.einsum("rc,rd->cd", context, mixed_grad, preferred_element_type=jnp.float32)
        context_grad = jnp.einsum(
            "rd,cd->rc", mixed_grad, out_full, preferred_element_type=jnp.float32
        )
        context_grad = context_grad.astype(jnp.bfloat16).reshape(
            block_count, QUERY_BLOCK, head_local, HEAD_DIM
        )
        zero_heads = jnp.zeros((row_count, head_local, HEAD_DIM), jnp.float32)
        (key_total, value_total), query_total = lax.scan(
            partial(attend_back, key_heads, value_heads, attention_scale),
            (zero_heads, zero_heads),
            (query_blocks, context_grad, same_blocks, log_total),
        )
        heads_grad = jnp.stack(
            [
                query_total.reshape(row_count, head_local * HEAD_DIM),
                key_total.reshape(row_count, head_local * HEAD_DIM),
                value_total.reshape(row_count, head_local * HEAD_DIM),
            ],
            axis=1,
        ).astype(jnp.bfloat16)
        head_bias_sum = head_bias_sum + jnp.stack(
            [
                jnp.sum(heads_grad[:, 0].astype(jnp.float32), axis=0),
                jnp.sum(heads_grad[:, 2].astype(jnp.float32), axis=0),
            ]
        )
        heads_term = jnp.einsum(
            "rd,rtc->dtc", first_normed, heads_grad, preferred_element_type=jnp.float32
        )
        first_normed_grad = lax.psum_scatter(
            heads_term_rows(heads_grad, heads_full).astype(jnp.bfloat16),
            "narrow",
            scatter_dimension=0,
            tiled=True,
        ).astype(jnp.float32)
        first_unit_part = quarter_rows(first_unit)
        first_gain_sum = first_gain_sum + jnp.sum(first_normed_grad * first_unit_part, axis=0)
        first_shift_sum = first_shift_sum + jnp.sum(first_normed_grad, axis=0)
        input_grads.append(
            (
                middle_grad
                + norm_back(
                    first_normed_grad, first_unit_part, quarter_rows(first_inverse), first_gain
                )
            ).astype(jnp.bfloat16)
        )
        term_list.append((heads_term, out_term, up_term, down_term))
    summed_terms = reduce(add_tuples, term_list)
    heads_total, out_total, up_total, down_total, head_bias_total, up_bias_total = lax.psum(
        (
            summed_terms[0],
            summed_terms[1],
            summed_terms[2],
            summed_terms[3],
            head_bias_sum,
            up_bias_sum,
        ),
        "wide",
    )
    (
        out_bias_total,
        down_bias_total,
        first_gain_total,
        first_shift_total,
        second_gain_total,
        second_shift_total,
        mixer_scale_total,
        feed_scale_total,
    ) = lax.psum(
        (
            out_bias_sum,
            down_bias_sum,
            first_gain_sum,
            first_shift_sum,
            second_gain_sum,
            second_shift_sum,
            mixer_scale_sum,
            feed_scale_sum,
        ),
        ("wide", "narrow"),
    )
    return (
        jnp.stack(outputs),
        jnp.stack(input_grads),
        heads_total,
        head_bias_total,
        out_total,
        out_bias_total,
        up_total,
        up_bias_total,
        down_total,
        down_bias_total,
        first_gain_total,
        first_shift_total,
        second_gain_total,
        second_shift_total,
        mixer_scale_total,
        feed_scale_total,
    )


def solution(mesh):
    return jax.shard_map(
        body,
        mesh=mesh,
        in_specs=(
            P(None, "wide", None),
            P(None, "wide", None),
            P("wide", None, "narrow"),
            P(None, "narrow"),
            P("narrow", "wide"),
            P(),
            P("wide", "narrow"),
            P("narrow"),
            P("narrow", "wide"),
            P(),
            P(),
            P(),
            P(),
            P(),
            P(),
            P(),
            P(None, "wide", None),
        ),
        out_specs=(
            P(None, "wide", None),
            P(None, ("wide", "narrow"), None),
            P(None, None, "narrow"),
            P(None, "narrow"),
            P("narrow", None),
            P(),
            P(None, "narrow"),
            P("narrow"),
            P("narrow", None),
            P(),
            P(),
            P(),
            P(),
            P(),
            P(),
            P(),
        ),
        check_vma=False,
    )
```

profile of v0, /device:TPU:0, one launch (start us, length us, event | category | flops | bytes accessed | tf_op | source)
XLA Modules:
  0.0 991.4 jit_solution(16991604911997666892)
XLA Ops:
  8.1 3.7 convert_reduce_fusion.2
  15.0 38.7 %all_gather.14 = bf16[768,3,192]{2,1,0:T(4,128)(2,1)S(1)} all-gather(bf16[96,3,192]{2,1,0:T(4,128)(2,1)S(1)} %copy.82), channel_id=1, replica_groups=mesh['wide'=8,'narrow'=4] {'wide'}, dimensions={0}, use_global_device_ids=true | all-gather | bytes 995328 | tf_op jit(solution)/shard_map/all_gather | solution.py:139
  54.6 3.8 fusion.231
  68.0 33.3 %all_gather.30 = bf16[192,768]{0,1:T(8,128)(2,1)} all-gather(bf16[192,96]{0,1:T(8,128)(2,1)S(1)} %copy.86), channel_id=1, replica_groups=mesh['wide'=8,'narrow'=4] {'wide'}, dimensions={1}, use_global_device_ids=true | all-gather | bytes 331776 | tf_op jit(solution)/shard_map/all_gather | solution.py:140
  120.0 23.4 %while.83 = (s32[]{:T(128)}, bf16[2,640,3,64]{1,3,2,0:T(8,128)(2,1)}, f32[2,3,640,1]{2,1,3,0:T(4,128)S(1)}, pred[2,640,1280]{2,1,0:T(8,128)(4,1)}, bf16[2,640,3,...) while((s32[]{:T(128)}, ...), condition=%wide.region_31.32_spmd, body=%wide.region_28.31_spmd.sunk | while | flops 658634880 | bytes 41280192 | solution.py:166
  121.8 3.2 fusion.390
  133.2 3.2 fusion.390
  139.4 3.2 fusion.392
  144.4 18.8 %while.82 = (s32[]{:T(128)}, bf16[2,640,3,64]{1,3,2,0:T(8,128)(2,1)}, f32[2,3,640,1]{2,1,3,0:T(4,128)S(1)}, pred[2,640,1280]{2,1,0:T(8,128)(4,1)S(1)}, bf16[2,64...) while((s32[]{:T(128)}, ...), condition=%wide.region_19.20_spmd, body=%wide.region_16.19_spmd.sunk | while | flops 658634880 | bytes 41280192 | solution.py:166
  159.2 3.2 fusion.387
  164.8 23.0 %while.81 = (s32[]{:T(128)}, bf16[2,640,3,64]{1,3,2,0:T(8,128)(2,1)}, f32[2,3,640,1]{2,1,3,0:T(4,128)S(1)}, pred[2,640,1280]{2,1,0:T(8,128)(4,1)}, bf16[2,640,3,...) while((s32[]{:T(128)}, ...), condition=%wide.region_7.8_spmd, body=%wide.region_4.7_spmd.sunk | while | flops 658634880 | bytes 41280192 | solution.py:166
  166.3 3.2 fusion.380
  172.4 3.2 fusion.382
  177.7 3.2 fusion.380
  199.3 111.8 %all-reduce.13.cloned.1.call-done = (bf16[1280,768]{1,0:T(8,128)(2,1)}, bf16[1280,768]{1,0:T(8,128)(2,1)}, bf16[1280,768]{1,0:T(8,128)(2,1)}) async-done(((bf16[1280,768]{1,0:T(8,128)(2,1)}, bf16[1280,768]{1,0:T(8,128)(2,1)}, bf16[1280,768]{1,0:T(8,128)(2,1)}), (bf16[1280,768]{1,0:T(8,128)(2,1)}, bf16[1280,768]{1,0:T(8,128)(2,1)}, bf16[1280,768]{1,0:T(8,128)(2,1)})) %all-reduce.13.cloned.1.call-update) | async-done | bytes 5898256 | tf_op jit(solution)/shard_map/psum | solution.py:171
  311.2 8.6 fusion.206
  321.8 3.9 multiply_reduce_fusion.5
  325.9 6.9 subtract_multiply_fusion.2
  332.8 13.9 %multiply_convert_fusion.5 = (bf16[1280,768]{1,0:T(8,128)(2,1)}, f32[1280,768]{1,0:T(8,128)}, f32[1280,768]{1,0:T(8,128)}) fusion(f32[768]{0:T(1024)S(1)} %copy-done.172, bf16[768,768]{1,0:T(8,128)(2,1)} %all-gather.6.cloned.1.call-done, f32[1280,768]{1,0:T(8,128)} %get-tuple-element.723, f32[768]{0:T(1024)S(1)} %copy-done.173, f32[768]{0:T(1024)S(1)} %copy-done.143), kind=kOutput, calls=%fused_computation.210 | convolution fusion | flops 1577779200 | bytes 14951424 | tf_op jit(solution)/shard_map/dot_general | solution.py:178
  346.8 7.7 convert_reduce_fusion.5
  358.9 12.5 %multiply_convert_fusion.4 = (bf16[1280,768]{1,0:T(8,128)(2,1)}, f32[1280,768]{1,0:T(8,128)S(1)}, f32[1280,768]{1,0:T(8,128)S(1)}) fusion(f32[768]{0:T(1024)S(1)} %copy-done.172, bf16[768,768]{1,0:T(8,128)(2,1)} %all-gather.6.cloned.1.call-done, f32[1280,768]{1,0:T(8,128)} %get-tuple-element.724, f32[768]{0:T(1024)S(1)} %copy-done.173, f32[768]{0:T(1024)S(1)} %copy-done.143), kind=kOutput, calls=%fused_computation.193 | convolution fusion | flops 1577779200 | bytes 14951424 | tf_op jit(solution)/shard_map/dot_general | solution.py:178
  371.4 5.2 convert_reduce_fusion.4
  381.0 12.8 %multiply_convert_fusion.3 = (bf16[1280,768]{1,0:T(8,128)(2,1)}, f32[1280,768]{1,0:T(8,128)S(1)}, f32[1280,768]{1,0:T(8,128)S(1)}) fusion(f32[768]{0:T(1024)S(1)} %copy-done.172, bf16[768,768]{1,0:T(8,128)(2,1)} %all-gather.6.cloned.1.call-done, f32[1280,768]{1,0:T(8,128)} %get-tuple-element.725, f32[768]{0:T(1024)S(1)} %copy-done.173, f32[768]{0:T(1024)S(1)} %copy-done.143), kind=kOutput, calls=%fused_computation.176 | convolution fusion | flops 1577779200 | bytes 14951424 | tf_op jit(solution)/shard_map/dot_general | solution.py:178
  393.8 5.2 convert_reduce_fusion.3
  403.4 7.5 slice_convert_fusion
  417.9 4.6 reduce-scatter.11.cloned.1.call-done
  422.6 33.4 %reduce-scatter.15.cloned.1.call-done = bf16[320,768]{1,0:T(8,128)(2,1)} async-done(((bf16[1280,768]{1,0:T(8,128)(2,1)}), bf16[320,768]{1,0:T(8,128)(2,1)}) %reduce-scatter.15.cloned.1.call-update) | async-done | bytes 491536 | tf_op jit(solution)/shard_map/reduce_scatter | solution.py:197
  456.0 3.9 fusion.196
  459.9 5.0 multiply_reduce_fusion.7
  473.4 4.8 convolution_convert_fusion.8
  484.7 4.7 convolution_convert_fusion.7
  492.5 4.6 fusion.226
  500.0 5.0 add_add_fusion
  505.0 3.4 add_add_fusion.1
  509.4 3.2 convolution_convert_fusion.9
  517.3 57.6 %while.86 = (s32[]{:T(128)}, f32[1280,3,64]{0,2,1:T(8,128)}, f32[1280,3,64]{0,2,1:T(8,128)}, bf16[2,640,3,64]{1,3,2,0:T(8,128)(2,1)}, bf16[2,640,3,64]{1,3,2,0:T...) while((s32[]{:T(128)}, f32[1280,3,64]{0,2,1:T(8,128)}, ...), condition=%wide.region_59.60_spmd.clone, body=%wide.region_57.59_spmd.clone.sunk | while | flops 1596332160 | bytes 153887056 | solution.py:229
  519.8 6.7 multiply_reduce_fusion.14
  526.6 9.8 multiply_convert_fusion.14
  536.5 5.8 fusion.430
  548.4 6.7 multiply_reduce_fusion.14
  555.1 10.0 %multiply_convert_fusion.14 = bf16[3,640,1280]{2,1,0:T(8,128)(2,1)} fusion(f32[3,640,1280]{2,1,0:T(8,128)} %get-tuple-element.1107, f32[3,640,1280]{2,1,0:T(8,128)} %copy-done, f32[3,640]{1,0:T(4,128)S(1)} %get-tuple-element.1108), kind=kLoop, calls=%fused_computation.104.clone.1 | loop fusion | flops 7372800 | bytes 24583680 | tf_op jit(solution)/shard_map/while/body/eval_jaxpr/convert_element_type | solution.py:68
  565.1 6.1 fusion.430
  574.8 3.3 convolution_convert_fusion.11
  582.8 4.5 bitcast_convert_fusion
  588.7 58.6 %while.84 = (s32[]{:T(128)}, f32[1280,3,64]{0,2,1:T(8,128)}, f32[1280,3,64]{0,2,1:T(8,128)}, bf16[2,640,3,64]{1,3,2,0:T(8,128)(2,1)}, bf16[2,640,3,64]{1,3,2,0:T...) while((s32[]{:T(128)}, f32[1280,3,64]{0,2,1:T(8,128)}, ...), condition=%wide.region_41.42_spmd.clone, body=%wide.region_39.41_spmd.clone.sunk | while | flops 1596332160 | bytes 153887056 | solution.py:229
  591.2 6.6 multiply_reduce_fusion.12
  597.8 11.1 %multiply_convert_fusion.12 = bf16[3,640,1280]{2,1,0:T(8,128)(2,1)} fusion(f32[3,640,1280]{2,1,0:T(8,128)} %get-tuple-element.1083, f32[3,640,1280]{2,1,0:T(8,128)} %copy-done.1, f32[3,640]{1,0:T(4,128)S(1)} %get-tuple-element.1084), kind=kLoop, calls=%fused_computation.48.clone.1 | loop fusion | flops 7372800 | bytes 24583680 | tf_op jit(solution)/shard_map/while/body/eval_jaxpr/convert_element_type | solution.py:68
  609.0 5.9 fusion.404
  621.0 6.6 multiply_reduce_fusion.12
  627.7 10.0 %multiply_convert_fusion.12 = bf16[3,640,1280]{2,1,0:T(8,128)(2,1)} fusion(f32[3,640,1280]{2,1,0:T(8,128)} %get-tuple-element.1083, f32[3,640,1280]{2,1,0:T(8,128)} %copy-done.1, f32[3,640]{1,0:T(4,128)S(1)} %get-tuple-element.1084), kind=kLoop, calls=%fused_computation.48.clone.1 | loop fusion | flops 7372800 | bytes 24583680 | tf_op jit(solution)/shard_map/while/body/eval_jaxpr/convert_element_type | solution.py:68
  637.6 6.0 fusion.404
  653.4 4.6 bitcast_convert_fusion.2
  659.1 58.0 %while.85 = (s32[]{:T(128)}, f32[1280,3,64]{0,2,1:T(8,128)}, f32[1280,3,64]{0,2,1:T(8,128)}, bf16[2,640,3,64]{1,3,2,0:T(8,128)(2,1)}, bf16[2,640,3,64]{1,3,2,0:T...) while((s32[]{:T(128)}, f32[1280,3,64]{0,2,1:T(8,128)}, ...), condition=%wide.region_50.51_spmd.clone, body=%wide.region_48.50_spmd.clone.sunk | while | flops 1596332160 | bytes 153887056 | solution.py:229
  661.6 6.6 multiply_reduce_fusion.13
  668.4 10.1 %multiply_convert_fusion.13 = bf16[3,640,1280]{2,1,0:T(8,128)(2,1)} fusion(f32[3,640,1280]{2,1,0:T(8,128)} %get-tuple-element.1095, f32[3,640,1280]{2,1,0:T(8,128)} %copy-done.2, f32[3,640]{1,0:T(4,128)S(1)} %get-tuple-element.1096), kind=kLoop, calls=%fused_computation.76.clone.1 | loop fusion | flops 7372800 | bytes 24583680 | tf_op jit(solution)/shard_map/while/body/eval_jaxpr/convert_element_type | solution.py:68
  678.4 5.9 fusion.417
  690.4 6.8 multiply_reduce_fusion.13
  697.6 9.8 multiply_convert_fusion.13
  707.4 6.1 fusion.417
  745.7 8.3 fusion.144
  758.3 23.9 %all-reduce.1 = (f32[2,192]{1,0:T(2,128)}, f32[768]{0:T(1024)}) all-reduce(f32[2,192]{1,0:T(2,128)S(1)} %fusion.235, f32[768]{0:T(1024)S(1)} %add_add_fusion.9), channel_id=1, replica_groups=mesh['wide'=8,'narrow'=4] {'wide'}, use_global_device_ids=true, to_apply=%region_70.71 | all-reduce | flops 1152 | bytes 9216 | tf_op jit(solution)/shard_map/psum | solution.py:270
  784.0 3.2 fusion.193
  790.4 41.3 %all-reduce = (f32[768]{0:T(1024)}, f32[768]{0:T(1024)}, f32[768]{0:T(1024)}, f32[768]{0:T(1024)}, f32[768]{0:T(1024)}, /*index=5*/f32[768]{0:T(1024)}, f32[768]{0:T(1024)}, f32[768]{0:T(1024)}) all-reduce(f32[768]{0:T(1024)S(1)} %add_multiply_fusion.1, ...), channel_id=1, replica_groups=mesh['wide'=8,'narrow'=4] {'wide','narrow'}, use_global_device_ids=true, to_apply=%region_75.76 | all-reduce | flops 6144 | bytes 49152 | tf_op jit(solution)/shard_map/psum | solution.py:290
  835.5 141.7 %all-reduce.9.cloned.1.call-done = (f32[768,3,192]{0,2,1:T(8,128)}, f32[192,768]{1,0:T(8,128)}, f32[768,768]{1,0:T(8,128)}, f32[768,768]{1,0:T(8,128)}) async-done(((f32[768,3,192]{0,2,1:T(8,128)}, f32[192,768]{1,0:T(8,128)}, f32[768,768]{1,0:T(8,128)}, f32[768,768]{1,0:T(8,128)}), (f32[768,3,192]{0,2,1:T(8,128)}, f32[192,768]{1,0:T(8,128)}, f32[768,768]{1,0:T(8,128)}, ...) | async-done | bytes 7077904 | tf_op jit(solution)/shard_map/psum | solution.py:270
  (695 shorter events, 233.7 us)
Async XLA Ops:
  8.0 303.1 %all-reduce.13.cloned.1.call-start = ((), (), s32[]{:S(2)}) async-start(), calls=%async_computation.19 | async-start | bytes 11796480 | tf_op jit(solution)/shard_map/psum | solution.py:171
  11.8 51.1 %copy-start.122 = (f32[1280]{0:T(1024)}, f32[1280]{0:T(1024)S(1)}, u32[]{:S(2)}) copy-start(f32[1280]{0:T(1024)S(1)} %broadcast_multiply_fusion.5) | copy-start | bytes 15364
  11.8 42.7 %copy-start.125 = (f32[1280]{0:T(1024)}, f32[1280]{0:T(1024)S(1)}, u32[]{:S(2)}) copy-start(f32[1280]{0:T(1024)S(1)} %get-tuple-element.769) | copy-start | bytes 15364
  11.9 48.0 %copy-start.128 = (f32[1280]{0:T(1024)}, f32[1280]{0:T(1024)S(1)}, u32[]{:S(2)}) copy-start(f32[1280]{0:T(1024)S(1)} %get-tuple-element.770) | copy-start | bytes 15364
  12.5 42.1 %copy-start.131 = (f32[768]{0:T(1024)S(1)}, f32[768]{0:T(1024)}, u32[]{:S(2)}) copy-start(f32[768]{0:T(1024)} %param.39) | copy-start | bytes 9220
  12.5 42.1 %copy-start.174 = (f32[768]{0:T(1024)S(1)}, f32[768]{0:T(1024)}, u32[]{:S(2)}) copy-start(f32[768]{0:T(1024)} %param.40) | copy-start | bytes 9220
  14.8 43.5 %copy-start.134 = (f32[1280]{0:T(1024)}, f32[1280]{0:T(1024)S(1)}, u32[]{:S(2)}) copy-start(f32[1280]{0:T(1024)S(1)} %add_rsqrt_fusion.1) | copy-start | bytes 15364
  54.5 8.4 copy-start.108
  144.4 19.7 %copy-start.9 = (bf16[1280,1,192]{0,2,1:T(8,128)(2,1)S(1)}, bf16[1280,1,192]{0,2,1:T(8,128)(2,1)}, u32[]{:S(2)}) copy-start(bf16[1280,1,192]{0,2,1:T(8,128)(2,1)} %slice.187) | copy-start | bytes 1474564
  196.0 115.2 %copy-start.117 = (f32[768]{0:T(1024)S(1)}, f32[768]{0:T(1024)}, u32[]{:S(2)}) copy-start(f32[768]{0:T(1024)} %param.43) | copy-start | bytes 9220
  196.0 115.2 %copy-start.120 = (f32[768]{0:T(1024)S(1)}, f32[768]{0:T(1024)}, u32[]{:S(2)}) copy-start(f32[768]{0:T(1024)} %param.34) | copy-start | bytes 9220
  196.0 115.1 %copy-start.126 = (f32[1280]{0:T(1024)S(1)}, f32[1280]{0:T(1024)}, u32[]{:S(2)}) copy-start(f32[1280]{0:T(1024)} %copy-done.125) | copy-start | bytes 15364
  196.0 115.1 %copy-start.129 = (f32[1280]{0:T(1024)S(1)}, f32[1280]{0:T(1024)}, u32[]{:S(2)}) copy-start(f32[1280]{0:T(1024)} %copy-done.128) | copy-start | bytes 15364
  196.0 115.1 %copy-start.135 = (f32[1280]{0:T(1024)S(1)}, f32[1280]{0:T(1024)}, u32[]{:S(2)}) copy-start(f32[1280]{0:T(1024)} %copy-done.134) | copy-start | bytes 15364
  196.0 115.1 %copy-start.138 = (f32[1280]{0:T(1024)S(1)}, f32[1280]{0:T(1024)}, u32[]{:S(2)}) copy-start(f32[1280]{0:T(1024)} %copy-done.137) | copy-start | bytes 15364
  198.0 134.7 %all-gather.6.cloned.1.call-start = ((), (), s32[]{:S(2)}) async-start(), calls=%async_computation.6 | async-start | bytes 1327104 | tf_op jit(solution)/shard_map/all_gather | solution.py:141
  198.6 148.1 %all-gather.8.cloned.1.call-start = ((), (), s32[]{:S(2)}) async-start(), calls=%async_computation.7 | async-start | bytes 1327104 | tf_op jit(solution)/shard_map/all_gather | solution.py:142
  199.2 218.7 %reduce-scatter.7.cloned.1.call-start = ((), (), s32[]{:S(2)}) async-start(), calls=%async_computation.8 | async-start | bytes 2457600 | tf_op jit(solution)/shard_map/reduce_scatter | solution.py:197
  311.1 8.7 slice-start.2
  311.1 8.7 slice-start.3
  311.2 9.4 copy-start.17
  311.2 10.1 %copy-start.19 = (bf16[1280,768]{1,0:T(8,128)(2,1)S(1)}, bf16[1280,768]{1,0:T(8,128)(2,1)}, u32[]{:S(2)}) copy-start(bf16[1280,768]{1,0:T(8,128)(2,1)} %get-tuple-element.697) | copy-start | bytes 5898244
  311.2 10.7 %copy-start.21 = (bf16[1280,768]{1,0:T(8,128)(2,1)S(1)}, bf16[1280,768]{1,0:T(8,128)(2,1)}, u32[]{:S(2)}) copy-start(bf16[1280,768]{1,0:T(8,128)(2,1)} %get-tuple-element.698) | copy-start | bytes 5898244
  325.8 6.9 copy-start.143
  325.8 6.9 copy-start.172
  325.9 6.9 copy-start.173
  332.8 14.0 %copy-start.145 = (f32[768]{0:T(1024)S(1)}, f32[768]{0:T(1024)}, u32[]{:S(2)}) copy-start(f32[768]{0:T(1024)} %param.44) | copy-start | bytes 9220
  346.8 9.0 copy-start.169
  358.9 63.7 %reduce-scatter.11.cloned.1.call-start = ((), (), s32[]{:S(2)}) async-start(), calls=%async_computation.11 | async-start | bytes 2457600 | tf_op jit(solution)/shard_map/reduce_scatter | solution.py:197
  358.9 12.5 %copy-start.168 = (bf16[768,768]{0,1:T(8,128)(2,1)S(1)}, bf16[768,768]{0,1:T(8,128)(2,1)}, u32[]{:S(2)}) copy-start(bf16[768,768]{0,1:T(8,128)(2,1)} %all-gather.8.cloned.1.call-done) | copy-start | bytes 3538948
  380.9 75.0 %reduce-scatter.15.cloned.1.call-start = ((), (), s32[]{:S(2)}) async-start(), calls=%async_computation.14 | async-start | bytes 2457600 | tf_op jit(solution)/shard_map/reduce_scatter | solution.py:197
  403.3 105.4 %all-gather.14.cloned.1.call-start = ((), (), s32[]{:S(2)}) async-start(), calls=%async_computation.15 | async-start | bytes 2457600 | tf_op jit(solution)/shard_map/all_gather | solution.py:218
  417.9 42.0 %copy-start.87 = (bf16[320,768]{1,0:T(8,128)(2,1)S(1)}, bf16[320,768]{1,0:T(8,128)(2,1)}, u32[]{:S(2)}) copy-start(bf16[320,768]{1,0:T(8,128)(2,1)} %reduce-scatter.7.cloned.1.call-done) | copy-start | bytes 1474564
  422.6 37.3 %copy-start.88 = (bf16[320,768]{1,0:T(8,128)(2,1)S(1)}, bf16[320,768]{1,0:T(8,128)(2,1)}, u32[]{:S(2)}) copy-start(bf16[320,768]{1,0:T(8,128)(2,1)} %reduce-scatter.11.cloned.1.call-done) | copy-start | bytes 1474564
  465.9 12.3 %slice-start.6 = ((s8[5898240]{0:T(1024)(128)(4,1)}), s8[1703936]{0:T(1024)(128)(4,1)S(1)}, s32[]{:S(2)}) async-start(s8[5898240]{0:T(1024)(128)(4,1)} %bitcast.559), calls=%async_computation.26 | async-start | bytes 3407872
  467.1 107.7 %all-gather.10.cloned.1.call-start = ((), (), s32[]{:S(2)}) async-start(), calls=%async_computation.9 | async-start | bytes 2457600 | tf_op jit(solution)/shard_map/all_gather | solution.py:218
  467.7 179.6 %all-gather.12.cloned.1.call-start = ((), (), s32[]{:S(2)}) async-start(), calls=%async_computation.12 | async-start | bytes 2457600 | tf_op jit(solution)/shard_map/all_gather | solution.py:218
  484.7 240.1 %all-reduce.11.cloned.1.call-start = ((), (), s32[]{:S(2)}) async-start(), calls=%async_computation.18 | async-start | bytes 11796480 | tf_op jit(solution)/shard_map/psum | solution.py:181
  508.4 8.9 copy-start.12
  508.4 8.8 copy-start.16
  508.4 8.8 copy-start.26
  508.4 8.8 copy-start.43
  508.4 8.8 copy-start.112
  508.4 273.7 %reduce-scatter.17.cloned.1.call-start = ((), (), s32[]{:S(2)}) async-start(), calls=%async_computation.16 | async-start | bytes 2457600 | tf_op jit(solution)/shard_map/reduce_scatter | solution.py:251
  519.8 6.8 copy-start
  548.4 6.7 copy-start
  574.8 6.9 copy-start.28
  574.8 7.0 copy-start.37
  587.4 196.5 %reduce-scatter.9.cloned.1.call-start = ((), (), s32[]{:S(2)}) async-start(), calls=%async_computation.10 | async-start | bytes 2457600 | tf_op jit(solution)/shard_map/reduce_scatter | solution.py:251
  621.0 6.7 copy-start.1
  658.0 129.3 %reduce-scatter.13.cloned.1.call-start = ((), (), s32[]{:S(2)}) async-start(), calls=%async_computation.13 | async-start | bytes 2457600 | tf_op jit(solution)/shard_map/reduce_scatter | solution.py:251
  661.6 6.8 copy-start.2
  690.4 7.2 copy-start.2
  719.1 12.8 %copy-start.74 = (bf16[1280,1,192]{0,2,1:T(8,128)(2,1)}, bf16[1280,1,192]{0,2,1:T(8,128)(2,1)S(1)}, u32[]{:S(2)}) copy-start(bf16[1280,1,192]{0,2,1:T(8,128)(2,1)S(1)} %stack_reshape.39) | copy-start | bytes 1474564
  720.5 11.4 %copy-start.72 = (bf16[1280,3,64]{0,2,1:T(8,128)(2,1)}, bf16[1280,3,64]{0,2,1:T(8,128)(2,1)S(1)}, u32[]{:S(2)}) copy-start(bf16[1280,3,64]{0,2,1:T(8,128)(2,1)S(1)} %convert.53) | copy-start | bytes 1474564
  724.5 252.7 %all-reduce.9.cloned.1.call-start = ((), (), s32[]{:S(2)}) async-start(), calls=%async_computation.17 | async-start | bytes 14155776 | tf_op jit(solution)/shard_map/psum | solution.py:270
  757.2 26.8 %copy-start.51 = (f32[320,768]{1,0:T(8,128)S(1)}, f32[320,768]{1,0:T(8,128)}, u32[]{:S(2)}) copy-start(f32[320,768]{1,0:T(8,128)} %copy-done.50) | copy-start | bytes 2949124
  757.2 26.8 %copy-start.161 = (f32[320]{0:T(512)S(1)}, f32[320]{0:T(512)}, u32[]{:S(2)}) copy-start(f32[320]{0:T(512)} %dynamic-slice.26) | copy-start | bytes 3844
  757.6 29.6 %copy-start.49 = (f32[320,768]{1,0:T(8,128)S(1)}, f32[320,768]{1,0:T(8,128)}, u32[]{:S(2)}) copy-start(f32[320,768]{1,0:T(8,128)} %copy-done.48) | copy-start | bytes 2949124
  757.6 29.6 %copy-start.160 = (f32[320]{0:T(512)S(1)}, f32[320]{0:T(512)}, u32[]{:S(2)}) copy-start(f32[320]{0:T(512)} %dynamic-slice.22) | copy-start | bytes 3844
  784.0 47.7 %copy-start.53 = (f32[320,768]{1,0:T(8,128)S(1)}, f32[320,768]{1,0:T(8,128)}, u32[]{:S(2)}) copy-start(f32[320,768]{1,0:T(8,128)} %copy-done.52) | copy-start | bytes 2949124
  784.0 47.7 %copy-start.162 = (f32[320]{0:T(512)S(1)}, f32[320]{0:T(512)}, u32[]{:S(2)}) copy-start(f32[320]{0:T(512)} %dynamic-slice.24) | copy-start | bytes 3844
  787.2 46.0 %copy-start.90 = (bf16[1,320,768]{2,1,0:T(8,128)(2,1)S(1)}, bf16[1,320,768]{2,1,0:T(8,128)(2,1)}, u32[]{:S(2)}) copy-start(bf16[1,320,768]{2,1,0:T(8,128)(2,1)} %get-tuple-element.739) | copy-start | bytes 1474564
  787.3 44.5 %copy-start.84 = (bf16[320,768]{1,0:T(8,128)(2,1)S(1)}, bf16[320,768]{1,0:T(8,128)(2,1)}, u32[]{:S(2)}) copy-start(bf16[320,768]{1,0:T(8,128)(2,1)} %reduce-scatter.13.cloned.1.call-done) | copy-start | bytes 1474564
  (171 other events, 538.6 us)
Sparse Core Ops, SparseCore 0:
  198.2 112.8 all-reduce.12
  359.0 30.5 reduce-scatter.6
  392.1 30.3 reduce-scatter.10
  425.5 30.3 reduce-scatter.14
  467.2 21.8 all-gather.13
  491.1 21.8 all-gather.9
  514.5 21.8 all-gather.11
  539.0 113.2 all-reduce.10
  654.8 30.5 reduce-scatter.16
  687.8 30.3 reduce-scatter.8
  724.6 30.2 reduce-scatter.12
Sparse Core Ops, SparseCore 1:
  200.7 40.8 all-gather.5
  243.6 39.8 all-gather.7
  744.3 232.9 all-reduce.8
where the time goes:
time: 999 us; the launch traced here: 991 us
  waiting for transfers between devices  293 us (29%)
  matrix products  284 us (28%)
  other arithmetic  175 us (18%)
  blocking collectives  137 us (14%)
  local copies, waits for them, and re-layouts  79.8 us (8%)
  between operations  17.9 us (2%)
    psum x1, waiting for transfers between devices, body(): lax.psum((summed_terms[0], summed_terms[1], summed_terms[2], summed_terms...  142 us
    psum x1, waiting for transfers between devices, body(): lax.psum(jnp.dot(context, out_full, preferred_element_type=jnp.float32).a...  112 us
    convert_element_type x6, other arithmetic, attend_back(): score_grad = (soft_weights * (weight_grad - row_delta)).astype(jnp.bfloat16)  60.8 us
    psum x1, blocking collectives, body(): lax.psum((out_bias_sum, down_bias_sum, first_gain_sum, first_shift_sum, s...  41.3 us
    dot_general x6, matrix products, attend_back(): jnp.einsum('qhc,khc->hqk', query_heads, key_heads, preferred_element_type...  40 us
    dot_general x3, matrix products, body(): jnp.dot(second_normed, up_full, preferred_element_type=jnp.float32)  39.2 us
    all_gather x1, blocking collectives, body(): lax.all_gather(heads_weight, 'wide', axis=0, tiled=True)  38.7 us
    reduce_scatter x3, waiting for transfers between devices, body(): lax.psum_scatter(feed_term(upper_grad, up_full).astype(jnp.bfloat16), 'na...  38 us
  transfers between devices with their start and end apart: 14, of which 4 were waited for; matrix products, arithmetic and copies ran while one was open for 38% of the time, Pallas kernels for 0%

commit v1 on v0

--- a/solution.py
+++ b/solution.py
@@ -168,9 +168,12 @@
             (query_blocks, same_blocks),
         )
         context = context_blocks.reshape(row_count, head_local * HEAD_DIM).astype(jnp.bfloat16)
-        mixed = lax.psum(
-            jnp.dot(context, out_full, preferred_element_type=jnp.float32).astype(jnp.bfloat16),
-            "narrow",
+
+        def frame_update(arr_in):
+            return jnp.sum(lax.all_gather(arr_in, "narrow"), 0)
+
+        mixed = frame_update(
+            jnp.dot(context, out_full, preferred_element_type=jnp.float32).astype(jnp.bfloat16)
         ).astype(jnp.float32)
         middle = token_rows + mixer_scale * (mixed + out_bias)
         second_unit, second_inverse = norm_parts(middle)

time: 999 us -> 1070 us (1.071)
  waiting for transfers between devices: 293 us -> 346 us
  other arithmetic: 175 us -> 194 us
    psum x1 -> x0, waiting for transfers between devices: 112 us -> none  [body(): lax.psum(jnp.dot(context, out_full, preferred_element_type=jnp.float32).a...]
    all_gather x0 -> x3, waiting for transfers between devices: none -> 105 us  [frame_update(): return jnp.sum(lax.all_gather(arr_in, 'narrow'), 0)]
    all_gather x1, waiting for transfers between devices: 0.03 us -> 27.7 us  [body(): lax.all_gather(down_weight, 'wide', axis=1, tiled=True)]
    reduce_sum x0 -> x3, other arithmetic: none -> 18.8 us  [frame_update(): return jnp.sum(lax.all_gather(arr_in, 'narrow'), 0)]
    psum x1, waiting for transfers between devices: 142 us -> 158 us  [body(): lax.psum((summed_terms[0], summed_terms[1], summed_terms[2], summed_terms...]
    all_gather x1, waiting for transfers between devices: 0.01 us -> 15.4 us  [body(): lax.all_gather(up_weight, 'wide', axis=0, tiled=True)]
    unnamed x346 -> x356, local copies, waits for them, and re-layouts: 29.4 us -> 34 us
  transfers between devices with their start and end apart: 14 -> 16, of which waited for: 4 -> 8; matrix products, arithmetic and copies ran while one was open for 38% -> 41% of each run, Pallas kernels for 0% -> 0%
where the time goes in v1:
time: 1070 us; the launch traced here: 1060 us
  waiting for transfers between devices  346 us (32%)
  matrix products  284 us (27%)
  other arithmetic  194 us (18%)
  blocking collectives  136 us (13%)
  local copies, waits for them, and re-layouts  80.8 us (8%)
  between operations  16.4 us (2%)
    psum x1, waiting for transfers between devices, body(): lax.psum((summed_terms[0], summed_terms[1], summed_terms[2], summed_terms...  158 us
    all_gather x3, waiting for transfers between devices, frame_update(): return jnp.sum(lax.all_gather(arr_in, 'narrow'), 0)  105 us
    convert_element_type x6, other arithmetic, attend_back(): score_grad = (soft_weights * (weight_grad - row_delta)).astype(jnp.bfloat16)  61.2 us
    psum x1, blocking collectives, body(): lax.psum((out_bias_sum, down_bias_sum, first_gain_sum, first_shift_sum, s...  42.3 us
    dot_general x6, matrix products, attend_back(): jnp.einsum('qhc,khc->hqk', query_heads, key_heads, preferred_element_type...  39.8 us
    all_gather x1, blocking collectives, body(): lax.all_gather(heads_weight, 'wide', axis=0, tiled=True)  38.7 us
    dot_general x3, matrix products, body(): jnp.dot(second_normed, up_full, preferred_element_type=jnp.float32)  38.5 us
    reduce_scatter x3, waiting for transfers between devices, body(): lax.psum_scatter(feed_term(upper_grad, up_full).astype(jnp.bfloat16), 'na...  37.6 us
  transfers between devices with their start and end apart: 16, of which 8 were waited for; matrix products, arithmetic and copies ran while one was open for 41% of the time, Pallas kernels for 0%

profile of v1, /device:TPU:0, one launch (start us, length us, event | category | flops | bytes accessed | tf_op | source)
XLA Modules:
  0.0 1060.0 jit_solution(14814149824895746084)
XLA Ops:
  7.2 3.7 convert_reduce_fusion.2
  14.2 38.7 %all_gather.47 = bf16[768,3,192]{2,1,0:T(4,128)(2,1)S(1)} all-gather(bf16[96,3,192]{2,1,0:T(4,128)(2,1)S(1)} %copy.82), channel_id=1, replica_groups=mesh['wide'=8,'narrow'=4] {'wide'}, dimensions={0}, use_global_device_ids=true | all-gather | bytes 995328 | tf_op jit(solution)/shard_map/all_gather | solution.py:139
  53.7 3.7 fusion.231
  60.9 31.2 %all_gather.48 = bf16[192,768]{0,1:T(8,128)(2,1)S(1)} all-gather(bf16[192,96]{0,1:T(8,128)(2,1)S(1)} %copy.86), channel_id=1, replica_groups=mesh['wide'=8,'narrow'=4] {'wide'}, dimensions={1}, use_global_device_ids=true | all-gather | bytes 331776 | tf_op jit(solution)/shard_map/all_gather | solution.py:140
  96.5 3.9 fusion.228
  106.0 3.7 fusion.225
  121.8 18.8 %while.83 = (s32[]{:T(128)}, bf16[2,640,3,64]{1,3,2,0:T(8,128)(2,1)}, f32[2,3,640,1]{2,1,3,0:T(4,128)S(1)}, pred[2,640,1280]{2,1,0:T(8,128)(4,1)S(1)}, bf16[2,64...) while((s32[]{:T(128)}, ...), condition=%wide.region_31.32_spmd, body=%wide.region_28.31_spmd.sunk | while | flops 658634880 | bytes 41280192 | solution.py:166
  149.0 18.6 %while.82 = (s32[]{:T(128)}, bf16[2,640,3,64]{1,3,2,0:T(8,128)(2,1)}, f32[2,3,640,1]{2,1,3,0:T(4,128)S(1)}, pred[2,640,1280]{2,1,0:T(8,128)(4,1)S(1)}, bf16[2,64...) while((s32[]{:T(128)}, ...), condition=%wide.region_19.20_spmd, body=%wide.region_16.19_spmd.sunk | while | flops 658634880 | bytes 41280192 | solution.py:166
  176.1 17.1 %while.81 = (s32[]{:T(128)}, bf16[2,640,3,64]{1,3,2,0:T(8,128)(2,1)S(1)}, f32[2,3,640,1]{2,1,3,0:T(4,128)S(1)}, pred[2,640,1280]{2,1,0:T(8,128)(4,1)S(1)}, bf16[...) while((s32[]{:T(128)}, ...), condition=%wide.region_7.8_spmd, body=%wide.region_4.7_spmd.sunk | while | flops 658634880 | bytes 37347976 | solution.py:166
  200.3 6.2 reduce_sum.645
  206.5 51.2 %all-gather.24.cloned.1.call-done = bf16[5120,768]{1,0:T(8,128)(2,1)} async-done(((bf16[1280,768]{1,0:T(8,128)(2,1)}), bf16[5120,768]{1,0:T(8,128)(2,1)}) %all-gather.24.cloned.1.call-update) | async-done | bytes 7864336 | tf_op jit(solution)/shard_map/all_gather | solution.py:173
  257.7 6.2 reduce_sum.639
  263.9 51.3 %all-gather.22.cloned.1.call-done = bf16[5120,768]{1,0:T(8,128)(2,1)} async-done(((bf16[1280,768]{1,0:T(8,128)(2,1)}), bf16[5120,768]{1,0:T(8,128)(2,1)}) %all-gather.22.cloned.1.call-update) | async-done | bytes 7864336 | tf_op jit(solution)/shard_map/all_gather | solution.py:173
  315.2 6.4 reduce_sum.633
  321.7 8.6 fusion.206
  332.1 3.9 multiply_reduce_fusion.5
  336.1 6.8 subtract_multiply_fusion.2
  343.0 15.4 %all-gather.12.cloned.1.call-done = bf16[768,768]{1,0:T(8,128)(2,1)} async-done(((bf16[96,768]{1,0:T(8,128)(2,1)}), bf16[768,768]{1,0:T(8,128)(2,1)}) %all-gather.12.cloned.1.call-update) | async-done | bytes 1179664 | tf_op jit(solution)/shard_map/all_gather | solution.py:141
  358.4 14.2 %multiply_convert_fusion.5 = (bf16[1280,768]{1,0:T(8,128)(2,1)}, f32[1280,768]{1,0:T(8,128)}, f32[1280,768]{1,0:T(8,128)}) fusion(f32[768]{0:T(1024)S(1)} %copy-done.175, bf16[768,768]{1,0:T(8,128)(2,1)} %all-gather.12.cloned.1.call-done, f32[1280,768]{1,0:T(8,128)} %get-tuple-element.720, f32[768]{0:T(1024)S(1)} %copy-done.176, f32[768]{0:T(1024)S(1)} %copy-done.145), kind=kOutput, calls=%fused_computation.210 | convolution fusion | flops 1577779200 | bytes 14951424 | tf_op jit(solution)/shard_map/dot_general | solution.py:181
  372.6 27.7 %all-gather.14.cloned.1.call-done = bf16[768,768]{0,1:T(8,128)(2,1)} async-done(((bf16[768,96]{0,1:T(8,128)(2,1)}), bf16[768,768]{0,1:T(8,128)(2,1)}) %all-gather.14.cloned.1.call-update) | async-done | bytes 1179664 | tf_op jit(solution)/shard_map/all_gather | solution.py:142
  400.2 7.7 convert_reduce_fusion.5
  412.4 12.1 %multiply_convert_fusion.4 = (bf16[1280,768]{1,0:T(8,128)(2,1)}, f32[1280,768]{1,0:T(8,128)S(1)}, f32[1280,768]{1,0:T(8,128)S(1)}) fusion(f32[768]{0:T(1024)S(1)} %copy-done.175, bf16[768,768]{1,0:T(8,128)(2,1)S(1)} %copy-done.174, f32[1280,768]{1,0:T(8,128)} %get-tuple-element.721, f32[768]{0:T(1024)S(1)} %copy-done.176, f32[768]{0:T(1024)S(1)} %copy-done.145), kind=kOutput, calls=%fused_computation.193 | convolution fusion | flops 1577779200 | bytes 14951424 | tf_op jit(solution)/shard_map/dot_general | solution.py:181
  424.5 5.1 convert_reduce_fusion.4
  433.9 12.2 %multiply_convert_fusion.3 = (bf16[1280,768]{1,0:T(8,128)(2,1)}, f32[1280,768]{1,0:T(8,128)S(1)}, f32[1280,768]{1,0:T(8,128)S(1)}) fusion(f32[768]{0:T(1024)S(1)} %copy-done.175, bf16[768,768]{1,0:T(8,128)(2,1)S(1)} %copy-done.174, f32[1280,768]{1,0:T(8,128)} %get-tuple-element.722, f32[768]{0:T(1024)S(1)} %copy-done.176, f32[768]{0:T(1024)S(1)} %copy-done.145), kind=kOutput, calls=%fused_computation.176 | convolution fusion | flops 1577779200 | bytes 14951424 | tf_op jit(solution)/shard_map/dot_general | solution.py:181
  446.2 5.1 convert_reduce_fusion.3
  455.6 7.6 slice_convert_fusion
  470.4 4.1 reduce-scatter.11.cloned.1.call-done
  474.5 33.5 %reduce-scatter.15.cloned.1.call-done = bf16[320,768]{1,0:T(8,128)(2,1)} async-done(((bf16[1280,768]{1,0:T(8,128)(2,1)}), bf16[320,768]{1,0:T(8,128)(2,1)}) %reduce-scatter.15.cloned.1.call-update) | async-done | bytes 491536 | tf_op jit(solution)/shard_map/reduce_scatter | solution.py:200
  508.0 3.9 fusion.196
  512.0 5.0 multiply_reduce_fusion.7
  525.7 4.8 convolution_convert_fusion.8
  537.0 4.7 convolution_convert_fusion.7
  544.8 4.6 fusion.226
  552.7 5.0 add_add_fusion
  557.8 3.4 add_add_fusion.1
  570.1 57.4 %while.86 = (s32[]{:T(128)}, f32[1280,3,64]{0,2,1:T(8,128)}, f32[1280,3,64]{0,2,1:T(8,128)}, bf16[2,640,3,64]{1,3,2,0:T(8,128)(2,1)}, bf16[2,640,3,64]{1,3,2,0:T...) while((s32[]{:T(128)}, f32[1280,3,64]{0,2,1:T(8,128)}, ...), condition=%wide.region_59.60_spmd.clone, body=%wide.region_57.59_spmd.clone.sunk | while | flops 1596332160 | bytes 153887056 | solution.py:232
  572.6 6.7 multiply_reduce_fusion.14
  579.3 9.8 multiply_convert_fusion.14
  589.2 5.8 fusion.430
  601.1 6.8 multiply_reduce_fusion.14
  607.9 9.9 multiply_convert_fusion.14
  617.8 6.1 fusion.430
  627.5 3.4 convolution_convert_fusion.11
  635.6 4.5 bitcast_convert_fusion
  641.2 58.7 %while.84 = (s32[]{:T(128)}, f32[1280,3,64]{0,2,1:T(8,128)}, f32[1280,3,64]{0,2,1:T(8,128)}, bf16[2,640,3,64]{1,3,2,0:T(8,128)(2,1)}, bf16[2,640,3,64]{1,3,2,0:T...) while((s32[]{:T(128)}, f32[1280,3,64]{0,2,1:T(8,128)}, ...), condition=%wide.region_41.42_spmd.clone, body=%wide.region_39.41_spmd.clone.sunk | while | flops 1596332160 | bytes 153887056 | solution.py:232
  643.8 6.6 multiply_reduce_fusion.12
  650.4 11.3 %multiply_convert_fusion.12 = bf16[3,640,1280]{2,1,0:T(8,128)(2,1)} fusion(f32[3,640,1280]{2,1,0:T(8,128)} %get-tuple-element.1080, f32[3,640,1280]{2,1,0:T(8,128)} %copy-done.1, f32[3,640]{1,0:T(4,128)S(1)} %get-tuple-element.1081), kind=kLoop, calls=%fused_computation.48.clone.1 | loop fusion | flops 7372800 | bytes 24583680 | tf_op jit(solution)/shard_map/while/body/eval_jaxpr/convert_element_type | solution.py:68
  661.7 5.9 fusion.404
  673.7 6.6 multiply_reduce_fusion.12
  680.3 10.0 multiply_convert_fusion.12
  690.3 6.0 fusion.404
  706.0 4.5 bitcast_convert_fusion.2
  711.9 58.3 %while.85 = (s32[]{:T(128)}, f32[1280,3,64]{0,2,1:T(8,128)}, f32[1280,3,64]{0,2,1:T(8,128)}, bf16[2,640,3,64]{1,3,2,0:T(8,128)(2,1)}, bf16[2,640,3,64]{1,3,2,0:T...) while((s32[]{:T(128)}, f32[1280,3,64]{0,2,1:T(8,128)}, ...), condition=%wide.region_50.51_spmd.clone, body=%wide.region_48.50_spmd.clone.sunk | while | flops 1596332160 | bytes 153887056 | solution.py:232
  714.4 6.6 multiply_reduce_fusion.13
  721.0 10.1 multiply_convert_fusion.13
  731.1 5.9 fusion.417
  743.1 6.6 multiply_reduce_fusion.13
  750.3 10.1 multiply_convert_fusion.13
  760.4 6.1 fusion.417
  798.9 7.5 fusion.144
  810.6 23.6 %all-reduce.1 = (f32[2,192]{1,0:T(2,128)}, f32[768]{0:T(1024)}) all-reduce(f32[2,192]{1,0:T(2,128)S(1)} %fusion.235, f32[768]{0:T(1024)S(1)} %add_add_fusion.9), channel_id=1, replica_groups=mesh['wide'=8,'narrow'=4] {'wide'}, use_global_device_ids=true, to_apply=%region_70.71 | all-reduce | flops 1152 | bytes 9216 | tf_op jit(solution)/shard_map/psum | solution.py:273
  836.0 3.3 fusion.193
  842.6 42.3 %all-reduce = (f32[768]{0:T(1024)}, f32[768]{0:T(1024)}, f32[768]{0:T(1024)}, f32[768]{0:T(1024)}, f32[768]{0:T(1024)}, /*index=5*/f32[768]{0:T(1024)}, f32[768]{0:T(1024)}, f32[768]{0:T(1024)}) all-reduce(f32[768]{0:T(1024)S(1)} %add_multiply_fusion.1, ...), channel_id=1, replica_groups=mesh['wide'=8,'narrow'=4] {'wide','narrow'}, use_global_device_ids=true, to_apply=%region_75.76 | all-reduce | flops 6144 | bytes 49152 | tf_op jit(solution)/shard_map/psum | solution.py:293
  888.7 158.0 %all-reduce.7.cloned.1.call-done = (f32[768,3,192]{0,2,1:T(8,128)}, f32[192,768]{1,0:T(8,128)}, f32[768,768]{1,0:T(8,128)}, f32[768,768]{1,0:T(8,128)}) async-done(((f32[768,3,192]{0,2,1:T(8,128)}, f32[192,768]{1,0:T(8,128)}, f32[768,768]{1,0:T(8,128)}, f32[768,768]{1,0:T(8,128)}), (f32[768,3,192]{0,2,1:T(8,128)}, f32[192,768]{1,0:T(8,128)}, f32[768,768]{1,0:T(8,128)}, ...) | async-done | bytes 7077904 | tf_op jit(solution)/shard_map/psum | solution.py:273
  (705 shorter events, 257.1 us)
Async XLA Ops:
  7.2 193.1 %all-gather.26.cloned.1.call-start = ((), (), s32[]{:S(2)}) async-start(), calls=%async_computation.19 | async-start | bytes 9830400 | tf_op jit(solution)/shard_map/all_gather | solution.py:173
  11.0 95.0 %copy-start.124 = (f32[1280]{0:T(1024)}, f32[1280]{0:T(1024)S(1)}, u32[]{:S(2)}) copy-start(f32[1280]{0:T(1024)S(1)} %broadcast_multiply_fusion.5) | copy-start | bytes 15364
  11.0 42.7 %copy-start.127 = (f32[1280]{0:T(1024)}, f32[1280]{0:T(1024)S(1)}, u32[]{:S(2)}) copy-start(f32[1280]{0:T(1024)S(1)} %get-tuple-element.766) | copy-start | bytes 15364
  11.0 85.4 %copy-start.130 = (f32[1280]{0:T(1024)}, f32[1280]{0:T(1024)S(1)}, u32[]{:S(2)}) copy-start(f32[1280]{0:T(1024)S(1)} %get-tuple-element.767) | copy-start | bytes 15364
  11.7 42.1 %copy-start.133 = (f32[768]{0:T(1024)S(1)}, f32[768]{0:T(1024)}, u32[]{:S(2)}) copy-start(f32[768]{0:T(1024)} %param.39) | copy-start | bytes 9220
  11.7 42.1 %copy-start.177 = (f32[768]{0:T(1024)S(1)}, f32[768]{0:T(1024)}, u32[]{:S(2)}) copy-start(f32[768]{0:T(1024)} %param.40) | copy-start | bytes 9220
  14.0 43.4 %copy-start.136 = (f32[1280]{0:T(1024)}, f32[1280]{0:T(1024)S(1)}, u32[]{:S(2)}) copy-start(f32[1280]{0:T(1024)S(1)} %add_rsqrt_fusion.1) | copy-start | bytes 15364
  60.8 45.2 %copy-start.142 = (f32[1280]{0:T(1024)}, f32[1280]{0:T(1024)S(1)}, u32[]{:S(2)}) copy-start(f32[1280]{0:T(1024)S(1)} %add_rsqrt_fusion.5) | copy-start | bytes 15364
  60.8 39.5 %copy-start.139 = (f32[1280]{0:T(1024)}, f32[1280]{0:T(1024)S(1)}, u32[]{:S(2)}) copy-start(f32[1280]{0:T(1024)S(1)} %add_rsqrt_fusion.3) | copy-start | bytes 15364
  92.1 101.8 %copy-start.49 = (bf16[192,768]{0,1:T(8,128)(2,1)}, bf16[192,768]{0,1:T(8,128)(2,1)S(1)}, u32[]{:S(2)}) copy-start(bf16[192,768]{0,1:T(8,128)(2,1)S(1)} %all_gather.48) | copy-start | bytes 884740
  140.6 7.5 copy-start.30
  140.6 8.3 copy-start.113
  145.5 112.2 %all-gather.24.cloned.1.call-start = ((), (), s32[]{:S(2)}) async-start(), calls=%async_computation.18 | async-start | bytes 9830400 | tf_op jit(solution)/shard_map/all_gather | solution.py:173
  168.2 7.9 copy-start.7
  173.0 142.2 %all-gather.22.cloned.1.call-start = ((), (), s32[]{:S(2)}) async-start(), calls=%async_computation.17 | async-start | bytes 9830400 | tf_op jit(solution)/shard_map/all_gather | solution.py:173
  193.2 13.2 %copy-start.11 = (bf16[1280,3,64]{0,2,1:T(8,128)(2,1)}, bf16[1280,3,64]{0,2,1:T(8,128)(2,1)S(1)}, u32[]{:S(2)}) copy-start(bf16[1280,3,64]{0,2,1:T(8,128)(2,1)S(1)} %get-tuple-element.1332) | copy-start | bytes 1474564
  193.3 13.2 %copy-start.24 = (pred[2,640,1280]{2,1,0:T(8,128)(4,1)}, pred[2,640,1280]{2,1,0:T(8,128)(4,1)S(1)}, u32[]{:S(2)}) copy-start(pred[2,640,1280]{2,1,0:T(8,128)(4,1)S(1)} %get-tuple-element.1335) | copy-start | bytes 4915204
  193.3 13.2 %copy-start.117 = (f32[2,3,640,1]{2,1,3,0:T(4,128)}, f32[2,3,640,1]{2,1,3,0:T(4,128)S(1)}, u32[]{:S(2)}) copy-start(f32[2,3,640,1]{2,1,3,0:T(4,128)S(1)} %get-tuple-element.1185) | copy-start | bytes 46084
  193.9 12.6 %copy-start.68 = (bf16[24,8,2,640]{3,1,2,0:T(8,128)(2,1)}, bf16[24,8,2,640]{3,1,2,0:T(8,128)(2,1)S(1)}, u32[]{:S(2)}) copy-start(bf16[24,8,2,640]{3,1,2,0:T(8,128)(2,1)S(1)} %copy.102) | copy-start | bytes 1474564
  195.9 162.5 %all-gather.12.cloned.1.call-start = ((), (), s32[]{:S(2)}) async-start(), calls=%async_computation.6 | async-start | bytes 1327104 | tf_op jit(solution)/shard_map/all_gather | solution.py:141
  196.5 203.8 %all-gather.14.cloned.1.call-start = ((), (), s32[]{:S(2)}) async-start(), calls=%async_computation.7 | async-start | bytes 1327104 | tf_op jit(solution)/shard_map/all_gather | solution.py:142
  197.1 273.3 %reduce-scatter.7.cloned.1.call-start = ((), (), s32[]{:S(2)}) async-start(), calls=%async_computation.8 | async-start | bytes 2457600 | tf_op jit(solution)/shard_map/reduce_scatter | solution.py:200
  315.2 15.2 %slice-start = ((s8[5898240]{0:T(1024)(128)(4,1)}), s8[1703936]{0:T(1024)(128)(4,1)S(1)}, s32[]{:S(2)}) async-start(s8[5898240]{0:T(1024)(128)(4,1)} %bitcast.552), calls=%async_computation.22 | async-start | bytes 3407872
  321.7 8.7 slice-start.1
  321.7 8.7 copy-start.13
  321.7 9.8 copy-start.16
  321.7 10.4 copy-start.18
  336.1 22.3 %copy-start.145 = (f32[768]{0:T(1024)S(1)}, f32[768]{0:T(1024)}, u32[]{:S(2)}) copy-start(f32[768]{0:T(1024)} %param.41) | copy-start | bytes 9220
  336.1 22.3 %copy-start.175 = (f32[768]{0:T(1024)S(1)}, f32[768]{0:T(1024)}, u32[]{:S(2)}) copy-start(f32[768]{0:T(1024)} %param.36) | copy-start | bytes 9220
  336.1 22.3 %copy-start.176 = (f32[768]{0:T(1024)S(1)}, f32[768]{0:T(1024)}, u32[]{:S(2)}) copy-start(f32[768]{0:T(1024)} %param.42) | copy-start | bytes 9220
  358.4 41.9 %copy-start.147 = (f32[768]{0:T(1024)S(1)}, f32[768]{0:T(1024)}, u32[]{:S(2)}) copy-start(f32[768]{0:T(1024)} %param.44) | copy-start | bytes 9220
  400.2 9.0 copy-start.174
  412.3 62.2 %reduce-scatter.11.cloned.1.call-start = ((), (), s32[]{:S(2)}) async-start(), calls=%async_computation.11 | async-start | bytes 2457600 | tf_op jit(solution)/shard_map/reduce_scatter | solution.py:200
  412.3 12.1 %copy-start.173 = (bf16[768,768]{0,1:T(8,128)(2,1)S(1)}, bf16[768,768]{0,1:T(8,128)(2,1)}, u32[]{:S(2)}) copy-start(bf16[768,768]{0,1:T(8,128)(2,1)} %all-gather.14.cloned.1.call-done) | copy-start | bytes 3538948
  433.9 74.1 %reduce-scatter.15.cloned.1.call-start = ((), (), s32[]{:S(2)}) async-start(), calls=%async_computation.14 | async-start | bytes 2457600 | tf_op jit(solution)/shard_map/reduce_scatter | solution.py:200
  455.6 105.9 %all-gather.20.cloned.1.call-start = ((), (), s32[]{:S(2)}) async-start(), calls=%async_computation.15 | async-start | bytes 2457600 | tf_op jit(solution)/shard_map/all_gather | solution.py:221
  455.6 7.6 copy-start.19
  470.4 41.5 %copy-start.92 = (bf16[320,768]{1,0:T(8,128)(2,1)S(1)}, bf16[320,768]{1,0:T(8,128)(2,1)}, u32[]{:S(2)}) copy-start(bf16[320,768]{1,0:T(8,128)(2,1)} %reduce-scatter.7.cloned.1.call-done) | copy-start | bytes 1474564
  474.5 37.5 %copy-start.93 = (bf16[320,768]{1,0:T(8,128)(2,1)S(1)}, bf16[320,768]{1,0:T(8,128)(2,1)}, u32[]{:S(2)}) copy-start(bf16[320,768]{1,0:T(8,128)(2,1)} %reduce-scatter.11.cloned.1.call-done) | copy-start | bytes 1474564
  517.9 12.6 %slice-start.4 = ((s8[5898240]{0:T(1024)(128)(4,1)}), s8[1703936]{0:T(1024)(128)(4,1)S(1)}, s32[]{:S(2)}) async-start(s8[5898240]{0:T(1024)(128)(4,1)} %bitcast.562), calls=%async_computation.26 | async-start | bytes 3407872
  519.2 108.3 %all-gather.16.cloned.1.call-start = ((), (), s32[]{:S(2)}) async-start(), calls=%async_computation.9 | async-start | bytes 2457600 | tf_op jit(solution)/shard_map/all_gather | solution.py:221
  519.8 180.1 %all-gather.18.cloned.1.call-start = ((), (), s32[]{:S(2)}) async-start(), calls=%async_computation.12 | async-start | bytes 2457600 | tf_op jit(solution)/shard_map/all_gather | solution.py:221
  537.0 240.9 %all-reduce.9.cloned.1.call-start = ((), (), s32[]{:S(2)}) async-start(), calls=%async_computation.21 | async-start | bytes 11796480 | tf_op jit(solution)/shard_map/psum | solution.py:184
  561.2 8.9 copy-start.10
  561.2 8.9 copy-start.23
  561.2 8.9 copy-start.31
  561.2 8.9 copy-start.48
  561.2 8.9 copy-start.114
  561.2 273.0 %reduce-scatter.17.cloned.1.call-start = ((), (), s32[]{:S(2)}) async-start(), calls=%async_computation.16 | async-start | bytes 2457600 | tf_op jit(solution)/shard_map/reduce_scatter | solution.py:254
  627.5 7.1 copy-start.42
  640.1 195.9 %reduce-scatter.9.cloned.1.call-start = ((), (), s32[]{:S(2)}) async-start(), calls=%async_computation.10 | async-start | bytes 2457600 | tf_op jit(solution)/shard_map/reduce_scatter | solution.py:254
  710.6 128.8 %reduce-scatter.13.cloned.1.call-start = ((), (), s32[]{:S(2)}) async-start(), calls=%async_computation.13 | async-start | bytes 2457600 | tf_op jit(solution)/shard_map/reduce_scatter | solution.py:254
  743.1 7.2 copy-start.2
  772.1 12.8 %copy-start.79 = (bf16[1280,1,192]{0,2,1:T(8,128)(2,1)}, bf16[1280,1,192]{0,2,1:T(8,128)(2,1)S(1)}, u32[]{:S(2)}) copy-start(bf16[1280,1,192]{0,2,1:T(8,128)(2,1)S(1)} %stack_reshape.39) | copy-start | bytes 1474564
  773.6 11.4 %copy-start.77 = (bf16[1280,3,64]{0,2,1:T(8,128)(2,1)}, bf16[1280,3,64]{0,2,1:T(8,128)(2,1)S(1)}, u32[]{:S(2)}) copy-start(bf16[1280,3,64]{0,2,1:T(8,128)(2,1)S(1)} %convert.56) | copy-start | bytes 1474564
  777.6 269.1 %all-reduce.7.cloned.1.call-start = ((), (), s32[]{:S(2)}) async-start(), calls=%async_computation.20 | async-start | bytes 14155776 | tf_op jit(solution)/shard_map/psum | solution.py:273
  809.5 26.5 %copy-start.56 = (f32[320,768]{1,0:T(8,128)S(1)}, f32[320,768]{1,0:T(8,128)}, u32[]{:S(2)}) copy-start(f32[320,768]{1,0:T(8,128)} %copy-done.55) | copy-start | bytes 2949124
  809.5 26.5 %copy-start.163 = (f32[320]{0:T(512)S(1)}, f32[320]{0:T(512)}, u32[]{:S(2)}) copy-start(f32[320]{0:T(512)} %dynamic-slice.26) | copy-start | bytes 3844
  810.0 29.4 %copy-start.54 = (f32[320,768]{1,0:T(8,128)S(1)}, f32[320,768]{1,0:T(8,128)}, u32[]{:S(2)}) copy-start(f32[320,768]{1,0:T(8,128)} %copy-done.53) | copy-start | bytes 2949124
  810.0 29.4 %copy-start.162 = (f32[320]{0:T(512)S(1)}, f32[320]{0:T(512)}, u32[]{:S(2)}) copy-start(f32[320]{0:T(512)} %dynamic-slice.22) | copy-start | bytes 3844
  836.0 48.8 %copy-start.58 = (f32[320,768]{1,0:T(8,128)S(1)}, f32[320,768]{1,0:T(8,128)}, u32[]{:S(2)}) copy-start(f32[320,768]{1,0:T(8,128)} %copy-done.57) | copy-start | bytes 2949124
  836.0 48.8 %copy-start.165 = (f32[320]{0:T(512)S(1)}, f32[320]{0:T(512)}, u32[]{:S(2)}) copy-start(f32[320]{0:T(512)} %dynamic-slice.24) | copy-start | bytes 3844
  839.3 47.0 %copy-start.95 = (bf16[1,320,768]{2,1,0:T(8,128)(2,1)S(1)}, bf16[1,320,768]{2,1,0:T(8,128)(2,1)}, u32[]{:S(2)}) copy-start(bf16[1,320,768]{2,1,0:T(8,128)(2,1)} %get-tuple-element.736) | copy-start | bytes 1474564
  839.4 45.5 %copy-start.89 = (bf16[320,768]{1,0:T(8,128)(2,1)S(1)}, bf16[320,768]{1,0:T(8,128)(2,1)}, u32[]{:S(2)}) copy-start(bf16[320,768]{1,0:T(8,128)(2,1)} %reduce-scatter.13.cloned.1.call-done) | copy-start | bytes 1474564
  (174 other events, 600.0 us)
Sparse Core Ops, SparseCore 0:
  145.6 54.5 all-gather.25
  202.4 55.2 all-gather.23
  259.9 55.2 all-gather.21
  317.2 41.1 all-gather.11
  360.4 39.8 all-gather.13
  412.4 29.0 reduce-scatter.6
  444.1 30.3 reduce-scatter.10
  477.6 30.3 reduce-scatter.14
  519.3 21.8 all-gather.19
  542.6 21.8 all-gather.15
  566.0 21.8 all-gather.17
  590.3 113.2 all-reduce.8
  706.2 30.5 reduce-scatter.16
  739.2 30.3 reduce-scatter.8
  777.7 30.4 reduce-scatter.12
  813.7 232.9 all-reduce.6
